TPU v7x, 32 devices: a whole 2x2x4 slice. The times are simulated.
32 devices in a mesh: rep: 4 (over x, y), dp: 8 (over z, core).
Axes of the slice: x: 2, y: 2, z: 4, core: 2. Of those that a mesh axis runs over, the one named last changes fastest.
Arguments:
- x: bfloat16 [32, 4096, 512], P(('rep', 'dp')), parts along dimension 0
- dy: bfloat16 [32, 4096, 512], P(('rep', 'dp')), parts along dimension 0
- w_gate: bfloat16 [2, 512, 1408], P(None, 'dp')
- w_up: bfloat16 [2, 512, 1408], P(None, 'dp')
- w_down: bfloat16 [2, 1408, 512], P(None, 'dp')
- m_w_gate: float32 [2, 512, 1408], P(None, 'dp')
- m_w_up: float32 [2, 512, 1408], P(None, 'dp')
- m_w_down: float32 [2, 1408, 512], P(None, 'dp')
- v_w_gate: float32 [2, 512, 1408], P(None, 'dp')
- v_w_up: float32 [2, 512, 1408], P(None, 'dp')
- v_w_down: float32 [2, 1408, 512], P(None, 'dp')
Outputs:
- output 1: bfloat16 [8, 512, 1408], P('rep', 'dp'), parts along dimension 0
- output 2: bfloat16 [8, 512, 1408], P('rep', 'dp'), parts along dimension 0
- output 3: bfloat16 [8, 1408, 512], P('rep', 'dp'), parts along dimension 0
- output 4: float32 [8, 512, 1408], P('rep', 'dp'), parts along dimension 0
- output 5: float32 [8, 512, 1408], P('rep', 'dp'), parts along dimension 0
- output 6: float32 [8, 1408, 512], P('rep', 'dp'), parts along dimension 0
- output 7: float32 [8, 512, 1408], P('rep', 'dp'), parts along dimension 0
- output 8: float32 [8, 512, 1408], P('rep', 'dp'), parts along dimension 0
- output 9: float32 [8, 1408, 512], P('rep', 'dp'), parts along dimension 0
There are 4 independent parts. A program takes and returns all parts, laid end to end along the dimension named above; an argument that names none is the same for every part.
All inputs are finite; a program needn't handle non-finite values.
Results may differ from a plain program's by a relative error of at most 0.022.
Values are sent between devices in bfloat16 or wider.
A program may use at most 2 GiB of HBM per device.

v0:
```python
import jax
import jax.numpy as jnp
from jax import lax
from jax.sharding import PartitionSpec as P

NAMES = ("w_gate", "w_up", "w_down")


def matmul(a, w):
    return jnp.dot(a, w, preferred_element_type=jnp.float32).astype(jnp.bfloat16)


def normed(h):
    wide = h.astype(jnp.float32)
    scale = lax.rsqrt(jnp.mean(wide**2, -1, keepdims=True) + 1e-6)
    return (wide * scale).astype(jnp.bfloat16)


def layer(h, w):
    a = normed(h)
    gate = jnp.dot(a, w["w_gate"], preferred_element_type=jnp.float32)
    up = jnp.dot(a, w["w_up"], preferred_element_type=jnp.float32)
    return h + matmul((jax.nn.silu(gate) * up).astype(jnp.bfloat16), w["w_down"])


def adamw(w, m, v, g):
    m = 0.9 * m + 0.1 * g
    v = 0.95 * v + 0.05 * g * g
    step = m * lax.rsqrt(v + 1e-8) + 0.1 * w
    return (w - 0.02 * step).astype(jnp.bfloat16), m, v


def clipped(gradients, sum_of_squares, count):
    factor = jnp.minimum(1.0, 0.5 * lax.rsqrt(sum_of_squares / count + 1e-30))
    return [g * factor for g in gradients]


def solution(mesh):
    def fetched(weights, number):
        return {name: lax.all_gather(w[number], "dp", axis=0, tiled=True) for name, w in zip(NAMES, weights, strict=True)}

    def step(x, dy, *arrays):
        weights, m, v = (arrays[i : i + 3] for i in (0, 3, 6))
        layers = weights[0].shape[0]
        h, kept = x[0], []
        for number in range(layers):
            kept.append(h)
            h = layer(h, fetched(weights, number))
        by_h, mine = dy[0], [None] * layers
        for number in reversed(range(layers)):
            _, back = jax.vjp(lambda w, h: layer(h, w), fetched(weights, number), kept[number])
            by_w, by_h = back(by_h)
            mine[number] = [lax.psum_scatter(by_w[name], "dp", scatter_dimension=0, tiled=True) for name in NAMES]
        gradients = [jnp.stack([mine[number][i] for number in range(layers)]).astype(jnp.float32) for i in range(3)]
        squares = lax.psum(sum(jnp.sum(g * g) for g in gradients), "dp")
        gradients = clipped(gradients, squares, lax.psum(1, "dp") * sum(g.size for g in gradients))
        new = [adamw(w.astype(jnp.float32), m, v, g) for w, m, v, g in zip(weights, m, v, gradients, strict=True)]
        return tuple(one[which] for which in range(3) for one in new)

    states, cut = P(("rep", "dp"), None, None), P(None, "dp", None)
    return jax.shard_map(
        step,
        mesh=mesh,
        in_specs=(states, states) + (cut,) * 9,
        out_specs=(P("rep", "dp", None),) * 9,
        check_vma=False,
    )
```

profile of v0, /device:TPU:0, one launch (start us, length us, event | category | flops | bytes accessed | tf_op | source)
XLA Modules:
  0.0 478.5 jit_solution(8858973093406137132)
XLA Ops:
  7.2 0.0 all-gather.13.cloned.1.call-start
  7.2 1.8 fusion.93
  9.0 0.0 all-gather.13.cloned.1.call-update
  9.0 0.0 all-gather.15.cloned.1.call-start
  9.1 1.8 fusion.92
  10.8 0.0 all-gather.15.cloned.1.call-update
  10.9 0.0 all-gather.17.cloned.1.call-start
  10.9 1.8 fusion.91
  12.7 0.0 all-gather.17.cloned.1.call-update
  12.7 0.0 all-gather.21.cloned.1.call-start
  12.7 0.5 all-gather.21.cloned.1.call-update
  13.3 0.0 all-gather.23.cloned.1.call-start
  13.3 0.5 all-gather.23.cloned.1.call-update
  13.9 0.0 all-gather.19.cloned.1.call-start
  13.9 0.5 all-gather.19.cloned.1.call-update
  14.4 0.0 reduce-scatter.9.cloned.1.call-start
  14.5 6.4 %copy.20 = bf16[1,4096,512]{1,2,0:T(8,128)(2,1)} copy(bf16[1,4096,512]{2,1,0:T(8,128)(2,1)} %param.11) | data formatting | bytes 8388608 | tf_op args[0]
  20.9 3.1 fusion.15
  24.0 6.4 %copy.21 = bf16[1,4096,512]{1,2,0:T(8,128)(2,1)} copy(bf16[1,4096,512]{2,1,0:T(8,128)(2,1)} %param.12) | data formatting | bytes 8388608 | tf_op args[1]
  30.4 6.7 %all-gather.13.cloned.1.call-done = bf16[1,512,1408]{2,1,0:T(8,128)(2,1)} async-done(((bf16[1,64,1408]{2,1,0:T(8,128)(2,1)}), bf16[1,512,1408]{2,1,0:T(8,128)(2,1)}) %all-gather.13.cloned.1.call-update) | async-done | bytes 1441808 | tf_op jit(solution)/shard_map/all_gather | solution.py:40
  37.2 13.2 %fusion.47 = f32[4096,1408]{1,0:T(8,128)} fusion(bf16[1,4096,512]{1,2,0:T(8,128)(2,1)} %copy.20, f32[4096]{0:T(1024)S(1)} %add_rsqrt_fusion, bf16[1,512,1408]{2,1,0:T(8,128)(2,1)} %all-gather.13.cloned.1.call-done), kind=kOutput, calls=%fused_computation.57 | convolution fusion | flops 5911871488 | bytes 28721152 | tf_op jit(solution)/shard_map/dot_general | solution.py:21
  50.4 12.8 %all-gather.15.cloned.1.call-done = bf16[1,512,1408]{2,1,0:T(8,128)(2,1)} async-done(((bf16[1,64,1408]{2,1,0:T(8,128)(2,1)}), bf16[1,512,1408]{2,1,0:T(8,128)(2,1)}) %all-gather.15.cloned.1.call-update) | async-done | bytes 1441808 | tf_op jit(solution)/shard_map/all_gather | solution.py:40
  63.2 24.3 %multiply_convert_fusion.1 = (bf16[4096,1408]{1,0:T(8,128)(2,1)}, f32[4096,1408]{1,0:T(8,128)}) fusion(f32[4096,1408]{1,0:T(8,128)} %fusion.47, bf16[1,512,1408]{2,1,0:T(8,128)(2,1)} %all-gather.15.cloned.1.call-done, bf16[1,4096,512]{1,2,0:T(8,128)(2,1)} %copy.20, f32[4096]{0:T(1024)S(1)} %add_rsqrt_fusion), kind=kOutput, calls=%fused_computation.17 | convolution fusion | flops 5946474496 | bytes 63324160 | tf_op jit(solution)/shard_map/dot_general | solution.py:22
  87.5 1.7 all-gather.17.cloned.1.call-done
  89.2 12.5 %fusion.19 = (f32[4096]{0:T(1024)S(1)}, bf16[4096,512]{0,1:T(8,128)(2,1)}) fusion(bf16[4096,1408]{1,0:T(8,128)(2,1)} %get-tuple-element.24, bf16[1,1408,512]{2,1,0:T(8,128)(2,1)} %all-gather.17.cloned.1.call-done, bf16[1,4096,512]{1,2,0:T(8,128)(2,1)} %copy.20), kind=kOutput, calls=%fused_computation.37 | convolution fusion | flops 5916061696 | bytes 21381120 | tf_op jit(solution)/shard_map/dot_general | solution.py:10
  101.7 0.6 copy-done.9
  102.3 12.7 %all-gather.21.cloned.1.call-done = bf16[1,1408,512]{2,1,0:T(8,128)(2,1)} async-done(((bf16[1,176,512]{2,1,0:T(8,128)(2,1)}), bf16[1,1408,512]{2,1,0:T(8,128)(2,1)}) %all-gather.21.cloned.1.call-update) | async-done | bytes 1441808 | tf_op jit(solution)/shard_map/all_gather | solution.py:40
  115.0 11.9 %convolution_convert_fusion.1 = bf16[4096,1408]{1,0:T(8,128)(2,1)} fusion(bf16[1,4096,512]{2,1,0:T(8,128)(2,1)} %param.12, bf16[1,1408,512]{2,1,0:T(8,128)(2,1)} %all-gather.21.cloned.1.call-done), kind=kOutput, calls=%fused_computation.23 | convolution fusion | flops 5911347200 | bytes 17170432 | tf_op jit(solution)/shard_map/transpose(jvp())/dot_general | solution.py:10
  127.0 13.9 %all-gather.23.cloned.1.call-done = bf16[1,512,1408]{2,1,0:T(8,128)(2,1)} async-done(((bf16[1,64,1408]{2,1,0:T(8,128)(2,1)}), bf16[1,512,1408]{2,1,0:T(8,128)(2,1)}) %all-gather.23.cloned.1.call-update) | async-done | bytes 1441808 | tf_op jit(solution)/shard_map/all_gather | solution.py:40
  140.9 13.1 %fusion.39 = f32[4096,1408]{1,0:T(8,128)} fusion(bf16[4096,512]{0,1:T(8,128)(2,1)} %get-tuple-element.27, f32[4096]{0:T(1024)S(1)} %fusion.79, bf16[1,512,1408]{2,1,0:T(8,128)(2,1)} %all-gather.23.cloned.1.call-done), kind=kOutput, calls=%fused_computation.54 | convolution fusion | flops 5911871488 | bytes 28721152 | tf_op jit(solution)/shard_map/jvp()/dot_general | solution.py:22
  154.0 12.8 %all-gather.19.cloned.1.call-done = bf16[1,512,1408]{2,1,0:T(8,128)(2,1)} async-done(((bf16[1,64,1408]{2,1,0:T(8,128)(2,1)}), bf16[1,512,1408]{2,1,0:T(8,128)(2,1)}) %all-gather.19.cloned.1.call-update) | async-done | bytes 1441808 | tf_op jit(solution)/shard_map/all_gather | solution.py:40
  166.7 31.8 %fusion.2 = (bf16[4096,1408]{1,0:T(8,128)(2,1)}, f32[4096,1408]{1,0:T(8,128)}) fusion(f32[4096,1408]{1,0:T(8,128)} %fusion.39, bf16[4096,1408]{1,0:T(8,128)(2,1)} %convolution_convert_fusion.1, bf16[1,512,1408]{2,1,0:T(8,128)(2,1)} %all-gather.19.cloned.1.call-done, bf16[4096,512]{0,1:T(8,128)(2,1)} %get-tuple-element.27, f32[4096]{0:T(1024)S(1)} %fusion.79), kind=kOutput, calls=%fused_computation.8 | convolution fusion | flops 5981077504 | bytes 74858496 | tf_op jit(solution)/shard_map/jvp()/dot_general | solution.py:21
  198.6 12.8 %convolution_convert_fusion.5 = bf16[512,1408]{1,0:T(8,128)(2,1)} fusion(bf16[4096,1408]{1,0:T(8,128)(2,1)} %get-tuple-element.28, bf16[4096,512]{0,1:T(8,128)(2,1)} %get-tuple-element.27, f32[4096]{0:T(1024)S(1)} %fusion.79), kind=kOutput, calls=%fused_computation.53 | convolution fusion | flops 5911871488 | bytes 17186816 | tf_op jit(solution)/shard_map/transpose(jvp())/dot_general | solution.py:21
  211.4 0.0 reduce-scatter.9.cloned.1.call-update
  211.4 0.0 reduce-scatter.7.cloned.1.call-start
  211.4 17.2 %fusion.22 = bf16[4096,512]{0,1:T(8,128)(2,1)} fusion(bf16[4096,1408]{1,0:T(8,128)(2,1)} %convolution_convert_fusion.1, bf16[1,512,1408]{2,1,0:T(8,128)(2,1)} %all-gather.23.cloned.1.call-done, f32[4096,1408]{1,0:T(8,128)} %get-tuple-element.29), kind=kOutput, calls=%fused_computation.40 | convolution fusion | flops 5942280192 | bytes 40239104 | tf_op jit(solution)/shard_map/transpose(jvp())/dot_general | solution.py:22
  228.7 11.1 %fusion.21 = (f32[4096]{0:T(1024)S(1)}, bf16[4096,512]{0,1:T(8,128)(2,1)S(1)}) fusion(bf16[4096,512]{0,1:T(8,128)(2,1)S(1)} %copy-done.1, bf16[4096,512]{0,1:T(8,128)(2,1)} %fusion.22, bf16[4096,1408]{1,0:T(8,128)(2,1)} %get-tuple-element.28, bf16[1,512,1408]{2,1,0:T(8,128)(2,1)} %all-gather.19.cloned.1.call-done), kind=kOutput, calls=%fused_computation.39 | convolution fusion | flops 5916061696 | bytes 25575424 | tf_op jit(solution)/shard_map/transpose(jvp())/dot_general | solution.py:21
  239.9 2.9 fusion.25
  242.8 9.5 %convolution_convert_fusion = bf16[4096,1408]{1,0:T(8,128)(2,1)} fusion(bf16[4096,512]{0,1:T(8,128)(2,1)S(1)} %fusion.25, bf16[1,1408,512]{2,1,0:T(8,128)(2,1)S(1)} %copy-done.13), kind=kOutput, calls=%fused_computation.22 | convolution fusion | flops 5911347200 | bytes 17170432 | tf_op jit(solution)/shard_map/transpose(jvp())/dot_general | solution.py:10
  252.3 24.5 %fusion.33 = bf16[512,1408]{1,0:T(8,128)(2,1)} fusion(f32[4096,1408]{1,0:T(8,128)} %fusion.47, f32[4096,1408]{1,0:T(8,128)} %get-tuple-element.25, bf16[4096,1408]{1,0:T(8,128)(2,1)} %convolution_convert_fusion, bf16[1,4096,512]{1,2,0:T(8,128)(2,1)} %copy.20, f32[4096]{0:T(1024)S(1)} %copy-done.12), kind=kOutput, calls=%fused_computation.50 | convolution fusion | flops 5976031232 | bytes 63324160 | tf_op jit(solution)/shard_map/transpose(jvp())/dot_general | solution.py:21
  276.9 0.0 reduce-scatter.7.cloned.1.call-update
  276.9 0.0 reduce-scatter.13.cloned.1.call-start
  276.9 17.3 %fusion.32 = bf16[512,1408]{1,0:T(8,128)(2,1)} fusion(bf16[4096,1408]{1,0:T(8,128)(2,1)} %convolution_convert_fusion.1, bf16[4096,512]{0,1:T(8,128)(2,1)} %get-tuple-element.27, f32[4096]{0:T(1024)S(1)} %fusion.79, f32[4096,1408]{1,0:T(8,128)} %get-tuple-element.29), kind=kOutput, calls=%fused_computation.49 | convolution fusion | flops 5947195392 | bytes 40255488 | tf_op jit(solution)/shard_map/transpose(jvp())/dot_general | solution.py:22
  294.2 0.0 reduce-scatter.13.cloned.1.call-update
  294.2 0.0 reduce-scatter.11.cloned.1.call-start
  294.3 17.6 %fusion.36 = bf16[512,1408]{1,0:T(8,128)(2,1)} fusion(bf16[4096,1408]{1,0:T(8,128)(2,1)} %convolution_convert_fusion, f32[4096,1408]{1,0:T(8,128)} %fusion.47, bf16[1,4096,512]{1,2,0:T(8,128)(2,1)} %copy.20, f32[4096]{0:T(1024)S(1)} %copy-done.12), kind=kOutput, calls=%fused_computation.51 | convolution fusion | flops 5947195392 | bytes 40255488 | tf_op jit(solution)/shard_map/transpose(jvp())/dot_general | solution.py:22
  311.9 0.0 reduce-scatter.11.cloned.1.call-update
  311.9 0.0 reduce-scatter.17.cloned.1.call-start
  312.0 20.4 %fusion.29 = bf16[1408,512]{1,0:T(8,128)(2,1)} fusion(bf16[1,4096,512]{2,1,0:T(8,128)(2,1)} %param.12, f32[4096,1408]{1,0:T(8,128)} %fusion.39, f32[4096,1408]{1,0:T(8,128)} %get-tuple-element.29), kind=kOutput, calls=%fused_computation.48 | convolution fusion | flops 5940903936 | bytes 51773440 | tf_op jit(solution)/shard_map/transpose(jvp())/dot_general | solution.py:10
  332.4 0.0 reduce-scatter.17.cloned.1.call-update
  332.5 0.0 reduce-scatter.15.cloned.1.call-start
  332.5 12.6 %convolution_convert_fusion.4 = bf16[1408,512]{1,0:T(8,128)(2,1)} fusion(bf16[4096,1408]{1,0:T(8,128)(2,1)} %get-tuple-element.24, bf16[4096,512]{0,1:T(8,128)(2,1)} %copy-done.2), kind=kOutput, calls=%fused_computation.52 | convolution fusion | flops 5906300928 | bytes 17170432 | tf_op jit(solution)/shard_map/transpose(jvp())/dot_general | solution.py:10
  345.1 0.0 reduce-scatter.15.cloned.1.call-update
  345.1 0.0 reduce-scatter.9.cloned.1.call-done
  345.2 0.0 reduce-scatter.7.cloned.1.call-done
  345.2 1.8 fusion.67
  347.0 31.9 %reduce-scatter.11.cloned.1.call-done = bf16[64,1408]{1,0:T(8,128)(2,1)} async-done(((bf16[512,1408]{1,0:T(8,128)(2,1)}), bf16[64,1408]{1,0:T(8,128)(2,1)}) %reduce-scatter.11.cloned.1.call-update) | async-done | bytes 180240 | tf_op jit(solution)/shard_map/reduce_scatter | solution.py:53
  378.9 1.8 fusion.68
  382.0 31.1 %reduce-scatter.17.cloned.1.call-done = bf16[176,512]{1,0:T(8,128)(2,1)} async-done(((bf16[1408,512]{1,0:T(8,128)(2,1)}), bf16[176,512]{1,0:T(8,128)(2,1)}) %reduce-scatter.17.cloned.1.call-update) | async-done | bytes 180240 | tf_op jit(solution)/shard_map/reduce_scatter | solution.py:53
  413.1 34.2 %reduce-scatter.15.cloned.1.call-done = bf16[176,512]{1,0:T(8,128)(2,1)} async-done(((bf16[1408,512]{1,0:T(8,128)(2,1)}), bf16[176,512]{1,0:T(8,128)(2,1)}) %reduce-scatter.15.cloned.1.call-update) | async-done | bytes 180240 | tf_op jit(solution)/shard_map/reduce_scatter | solution.py:53
  447.3 1.8 fusion.69
  449.8 14.5 %psum.7 = f32[]{:T(128)} all-reduce(f32[]{:T(128)S(6)} %add.99), channel_id=1, replica_groups=mesh['rep'=4,'dp'=8] {'dp'}, use_global_device_ids=true, to_apply=%region_12.13 | all-reduce | flops 1 | bytes 8 | tf_op jit(solution)/shard_map/psum | solution.py:55
  465.0 2.4 fusion.75
  467.4 4.0 fusion.66
  (31 shorter events, 0.1 us)
Async XLA Ops:
  7.2 30.0 %all-gather.13.cloned.1.call-start = ((), (), s32[]{:S(2)}) async-start(), calls=%async_computation.12 | async-start | bytes 1622016 | tf_op jit(solution)/shard_map/all_gather | solution.py:40
  9.0 54.1 %all-gather.15.cloned.1.call-start = ((), (), s32[]{:S(2)}) async-start(), calls=%async_computation.13 | async-start | bytes 1622016 | tf_op jit(solution)/shard_map/all_gather | solution.py:40
  10.9 78.3 %all-gather.17.cloned.1.call-start = ((), (), s32[]{:S(2)}) async-start(), calls=%async_computation.14 | async-start | bytes 1622016 | tf_op jit(solution)/shard_map/all_gather | solution.py:40
  12.7 102.3 %all-gather.21.cloned.1.call-start = ((), (), s32[]{:S(2)}) async-start(), calls=%async_computation.16 | async-start | bytes 1622016 | tf_op jit(solution)/shard_map/all_gather | solution.py:40
  13.3 127.6 %all-gather.23.cloned.1.call-start = ((), (), s32[]{:S(2)}) async-start(), calls=%async_computation.17 | async-start | bytes 1622016 | tf_op jit(solution)/shard_map/all_gather | solution.py:40
  13.9 152.9 %all-gather.19.cloned.1.call-start = ((), (), s32[]{:S(2)}) async-start(), calls=%async_computation.15 | async-start | bytes 1622016 | tf_op jit(solution)/shard_map/all_gather | solution.py:40
  14.4 330.7 %reduce-scatter.9.cloned.1.call-start = ((), (), s32[]{:S(2)}) async-start(), calls=%async_computation.7 | async-start | bytes 1622016 | tf_op jit(solution)/shard_map/reduce_scatter | solution.py:53
  24.0 39.2 %copy-start.11 = (f32[4096]{0:T(1024)}, f32[4096]{0:T(1024)S(1)}, u32[]{:S(2)}) copy-start(f32[4096]{0:T(1024)S(1)} %add_rsqrt_fusion) | copy-start | bytes 49156
  101.7 0.6 copy-start.9
  211.4 133.8 %reduce-scatter.7.cloned.1.call-start = ((), (), s32[]{:S(2)}) async-start(), calls=%async_computation.6 | async-start | bytes 1622016 | tf_op jit(solution)/shard_map/reduce_scatter | solution.py:53
  211.4 17.3 %copy-start.1 = (bf16[4096,512]{0,1:T(8,128)(2,1)S(1)}, bf16[4096,512]{0,1:T(8,128)(2,1)}, u32[]{:S(2)}) copy-start(bf16[4096,512]{0,1:T(8,128)(2,1)} %get-tuple-element.27) | copy-start | bytes 12582916
  228.7 11.2 %copy-start.10 = (f32[4096]{0:T(1024)S(1)}, f32[4096]{0:T(1024)}, u32[]{:S(2)}) copy-start(f32[4096]{0:T(1024)} %copy-done.9) | copy-start | bytes 49156
  228.7 11.2 %copy-start = (bf16[1,4096,512]{1,2,0:T(8,128)(2,1)S(1)}, bf16[1,4096,512]{1,2,0:T(8,128)(2,1)}, u32[]{:S(2)}) copy-start(bf16[1,4096,512]{1,2,0:T(8,128)(2,1)} %copy.21) | copy-start | bytes 12582916
  239.9 2.9 copy-start.13
  242.8 9.5 %copy-start.2 = (bf16[4096,512]{0,1:T(8,128)(2,1)}, bf16[4096,512]{0,1:T(8,128)(2,1)S(1)}, u32[]{:S(2)}) copy-start(bf16[4096,512]{0,1:T(8,128)(2,1)S(1)} %fusion.25) | copy-start | bytes 12582916
  242.8 9.5 %copy-start.12 = (f32[4096]{0:T(1024)S(1)}, f32[4096]{0:T(1024)}, u32[]{:S(2)}) copy-start(f32[4096]{0:T(1024)} %copy-done.11) | copy-start | bytes 49156
  276.9 70.1 %reduce-scatter.13.cloned.1.call-start = ((), (), s32[]{:S(2)}) async-start(), calls=%async_computation.9 | async-start | bytes 1622016 | tf_op jit(solution)/shard_map/reduce_scatter | solution.py:53
  294.2 84.7 %reduce-scatter.11.cloned.1.call-start = ((), (), s32[]{:S(2)}) async-start(), calls=%async_computation.8 | async-start | bytes 1622016 | tf_op jit(solution)/shard_map/reduce_scatter | solution.py:53
  311.9 101.2 %reduce-scatter.17.cloned.1.call-start = ((), (), s32[]{:S(2)}) async-start(), calls=%async_computation.11 | async-start | bytes 1622016 | tf_op jit(solution)/shard_map/reduce_scatter | solution.py:53
  332.4 132.5 %copy-start.5 = (bf16[2,176,512]{2,1,0:T(8,128)(2,1)S(1)}, bf16[2,176,512]{2,1,0:T(8,128)(2,1)}, u32[]{:S(2)}) copy-start(bf16[2,176,512]{2,1,0:T(8,128)(2,1)} %param.15) | copy-start | bytes 1081348
  332.4 132.5 %copy-start.6 = (f32[2,176,512]{2,1,0:T(8,128)S(1)}, f32[2,176,512]{2,1,0:T(8,128)}, u32[]{:S(2)}) copy-start(f32[2,176,512]{2,1,0:T(8,128)} %param.21) | copy-start | bytes 2162692
  332.4 132.5 %copy-start.7 = (f32[2,176,512]{2,1,0:T(8,128)S(1)}, f32[2,176,512]{2,1,0:T(8,128)}, u32[]{:S(2)}) copy-start(f32[2,176,512]{2,1,0:T(8,128)} %param.18) | copy-start | bytes 2162692
  332.5 135.0 %copy-start.3 = (bf16[2,64,1408]{2,1,0:T(8,128)(2,1)S(1)}, bf16[2,64,1408]{2,1,0:T(8,128)(2,1)}, u32[]{:S(2)}) copy-start(bf16[2,64,1408]{2,1,0:T(8,128)(2,1)} %param.13) | copy-start | bytes 1081348
  332.5 134.9 %copy-start.4 = (bf16[2,64,1408]{2,1,0:T(8,128)(2,1)S(1)}, bf16[2,64,1408]{2,1,0:T(8,128)(2,1)}, u32[]{:S(2)}) copy-start(bf16[2,64,1408]{2,1,0:T(8,128)(2,1)} %param.14) | copy-start | bytes 1081348
  332.5 134.9 %copy-start.8 = (f32[2,64,1408]{2,1,0:T(8,128)S(1)}, f32[2,64,1408]{2,1,0:T(8,128)}, u32[]{:S(2)}) copy-start(f32[2,64,1408]{2,1,0:T(8,128)} %param.19) | copy-start | bytes 2162692
  332.5 114.8 %reduce-scatter.15.cloned.1.call-start = ((), (), s32[]{:S(2)}) async-start(), calls=%async_computation.10 | async-start | bytes 1622016 | tf_op jit(solution)/shard_map/reduce_scatter | solution.py:53
Sparse Core Ops, SparseCore 0:
  10.2 26.9 all-gather.12
  39.4 23.7 all-gather.14
  65.4 23.7 all-gather.16
  91.2 23.7 all-gather.20
  117.1 23.7 all-gather.22
  142.9 23.7 all-gather.18
  211.5 33.2 reduce-scatter.8
  277.0 33.1 reduce-scatter.6
  312.5 32.1 reduce-scatter.12
  346.8 32.0 reduce-scatter.10
  381.2 31.8 reduce-scatter.16
  415.3 31.9 reduce-scatter.14
where the time goes:
time: 488 us; the launch traced here: 478 us
  matrix products  250 us (51%)
  waiting for transfers between devices  160 us (33%)
  local copies, waits for them, and re-layouts  18.8 us (4%)
  other arithmetic  17.8 us (4%)
  between operations  17.3 us (4%)
  blocking collectives  14.5 us (3%)
    reduce_scatter x6, waiting for transfers between devices, step(): lax.psum_scatter(by_w[name], 'dp', scatter_dimension=0, tiled=True)  97.3 us
    dot_general x5, matrix products, layer(): gate = jnp.dot(a, w['w_gate'], preferred_element_type=jnp.float32)  93.5 us
    dot_general x5, matrix products, layer(): up = jnp.dot(a, w['w_up'], preferred_element_type=jnp.float32)  89.5 us
    dot_general x5, matrix products, matmul(): jnp.dot(a, w, preferred_element_type=jnp.float32).astype(jnp.bfloat16)  67 us
    all_gather x6, waiting for transfers between devices, fetched(): lax.all_gather(w[number], 'dp', axis=0, tiled=True)  60.6 us
    psum x1, blocking collectives, step(): squares = lax.psum(sum((jnp.sum(g * g) for g in gradients)), 'dp')  14.5 us
    unnamed x30, local copies, waits for them, and re-layouts  13.5 us
  transfers between devices with their start and end apart: 12, of which 9 were waited for; matrix products, arithmetic and copies ran while one was open for 48% of the time, Pallas kernels for 0%

commit v1 on v0

v1 whole, which is shorter than its diff:
```python
import functools

import jax
import jax.numpy as jnp
from jax import lax
from jax.experimental import pallas as pl
from jax.experimental.pallas import tpu as pltpu
from jax.sharding import PartitionSpec as P

MESH = pl.DeviceIdType.MESH
F32, BF16 = jnp.float32, jnp.bfloat16
T, D, FF = 4096, 512, 1408
DEV = 8
C = 256
NK = 6
NJ = 2 * NK
SH = C // DEV
ROWS = 192
TB = 512
NT = T // TB


def normed(wide):
    scale = lax.rsqrt(jnp.mean(wide * wide, -1, keepdims=True) + 1e-6)
    return (wide * scale).astype(BF16)


def dot(a, b):
    return jnp.dot(a, b, preferred_element_type=F32)


def kernel(
    x_hbm, dy_hbm, p_hbm, g_out, sq_out,
    wbuf, a0, a1, at, by, byt, h1, acc, wgu, wd, wdt, wt, gd, ggu, pg, rx, tx, rl, rz, sq, nb,
    local_sem, s1_send, s1_recv, s2_send, s2_recv, s3_send, s3_recv,
    d_send, d_recv, z_send, z_recv, r_recv, n_send, n_recv,
):
    rep, dp = lax.axis_index("rep"), lax.axis_index("dp")
    z, c = dp // 2, dp % 2
    partner = z * 2 + (1 - c)
    outer = (z == 0) | (z == 3)
    inner = (z == 1) | (z == 2)
    near, far, opposite = 1 + z // 3, 2 - z // 3, 3 - z
    other_outer = 3 * (z - 1)
    other_outer = jnp.where(inner, other_outer, 0)
    far_outer = 3 - other_outer

    copies = [
        pltpu.make_async_copy(p_hbm, wbuf.at[:, c, z], local_sem.at[0]),
        pltpu.make_async_copy(x_hbm, h1, local_sem.at[1]),
        pltpu.make_async_copy(dy_hbm, by, local_sem.at[2]),
    ]
    for copy in copies:
        copy.start()
    barrier = pltpu.get_barrier_semaphore()
    for i in range(1, DEV):
        pl.semaphore_signal(barrier, inc=1, device_id=(rep, (dp + i) % DEV), device_id_type=MESH)
    for i in range(1, 4):
        pl.semaphore_signal(barrier, inc=1, device_id=((rep + i) % 4, dp), device_id_type=MESH)
    pl.semaphore_wait(barrier, DEV - 1 + 3)

    def quarter(j, zz, rr):
        return wbuf.at[j, c, zz, pl.ds(pl.multiple_of(rr * (ROWS // 4), 16), ROWS // 4)]

    def along_z(j, i):
        ref = quarter(j, z, rep)
        return pltpu.make_async_remote_copy(
            src_ref=ref, dst_ref=ref, send_sem=s1_send.at[j, i - 1], recv_sem=s1_recv.at[j, i - 1],
            device_id=(rep, ((z + i) % 4) * 2 + c), device_id_type=MESH)

    def from_z(j, i):
        ref = quarter(j, (z + 4 - i) % 4, rep)
        return pltpu.make_async_remote_copy(
            src_ref=ref, dst_ref=ref, send_sem=s1_send.at[j, i - 1], recv_sem=s1_recv.at[j, i - 1],
            device_id=(rep, dp), device_id_type=MESH)

    def across(j, i, q):
        ref = quarter(j, (z + 4 - i) % 4, rep)
        return pltpu.make_async_remote_copy(
            src_ref=ref, dst_ref=ref, send_sem=s2_send.at[j, i - 1, q - 1], recv_sem=s2_recv.at[j, i - 1, q - 1],
            device_id=((rep + q) % 4, dp), device_id_type=MESH)

    def from_across(j, i, q):
        ref = quarter(j, (z + 4 - i) % 4, (rep + 4 - q) % 4)
        return pltpu.make_async_remote_copy(
            src_ref=ref, dst_ref=ref, send_sem=s2_send.at[j, i - 1, q - 1], recv_sem=s2_recv.at[j, i - 1, q - 1],
            device_id=(rep, dp), device_id_type=MESH)

    def to_partner(j):
        ref = wbuf.at[j, c]
        return pltpu.make_async_remote_copy(
            src_ref=ref, dst_ref=ref, send_sem=s3_send.at[j], recv_sem=s3_recv.at[j],
            device_id=(rep, partner), device_id_type=MESH)

    def from_partner(j):
        ref = wbuf.at[j, 1 - c]
        return pltpu.make_async_remote_copy(
            src_ref=ref, dst_ref=ref, send_sem=s3_send.at[j], recv_sem=s3_recv.at[j],
            device_id=(rep, dp), device_id_type=MESH)

    def stage_one(j):
        for i in (1, 2, 3):
            along_z(j, i).start()

    def stage_two(j):
        for i in (1, 2, 3):
            from_z(j, i).wait_recv()
            for q in (1, 2, 3):
                across(j, i, q).start()

    def stage_three(j):
        for i in (1, 2, 3):
            for q in (1, 2, 3):
                from_across(j, i, q).wait_recv()
        to_partner(j).start()

    copies[0].wait()
    lax.fori_loop(0, NJ, lambda j, _: (stage_one(j), 0)[1], 0)

    def exchange(q):
        return pltpu.make_async_remote_copy(
            src_ref=pg.at[q % 2, 1 - c], dst_ref=rx.at[q], send_sem=d_send.at[q], recv_sem=d_recv.at[q],
            device_id=(rep, partner), device_id_type=MESH)

    def z_copy(q, block, dst, recv_sem, n, zz):
        return pltpu.make_async_remote_copy(
            src_ref=tx.at[q % 2, block], dst_ref=dst, send_sem=z_send.at[q, n], recv_sem=recv_sem,
            device_id=(rep, zz * 2 + c), device_id_type=MESH)

    def chip_sum(q, block):
        return pg[q % 2, c, block].astype(F32) + rx[q, block].astype(F32)

    def wait_z_sends(q):
        for n in range(3):
            z_copy(q, 0, rz.at[q, 0], z_recv.at[q, 0], n, z).wait_send()

    def rs_chip(q):
        exchange(q).wait_recv()

        @pl.when(q >= 2)
        def _():
            wait_z_sends(q - 2)

        for block in range(4):
            tx[q % 2, block] = chip_sum(q, block).astype(BF16)

        @pl.when(outer)
        def _():
            z_copy(q, opposite, rl.at[q], r_recv.at[q], 0, near).start()
            z_copy(q, far, rz.at[q, 1], z_recv.at[q, 1], 1, far).start()
            z_copy(q, near, rz.at[q, 0], z_recv.at[q, 0], 2, near).start()

        @pl.when(inner)
        def _():
            z_copy(q, opposite, rz.at[q, 2], z_recv.at[q, 2], 0, opposite).start()
            z_copy(q, other_outer, rz.at[q, 0], z_recv.at[q, 0], 1, other_outer).start()

    def rs_relay(q):
        @pl.when(inner)
        def _():
            z_copy(q, 0, rl.at[q], r_recv.at[q], 2, z).wait_recv()
            tx[q % 2, far_outer] = (chip_sum(q, far_outer) + rl[q].astype(F32)).astype(BF16)
            z_copy(q, far_outer, rz.at[q, 1], z_recv.at[q, 1], 2, far_outer).start()

    def rs_final(q):
        for n in range(2):
            z_copy(q, 0, rz.at[q, n], z_recv.at[q, n], 0, z).wait_recv()
        total = chip_sum(q, z) + rz[q, 0].astype(F32) + rz[q, 1].astype(F32)

        def finish(value):
            rounded = value.astype(BF16)
            g_out[q] = rounded
            wide = rounded.astype(F32)
            sq[...] += jnp.sum((wide * wide).reshape(ROWS // 8, 8, C), 0)

        @pl.when(outer)
        def _():
            finish(total)

        @pl.when(inner)
        def _():
            z_copy(q, 0, rz.at[q, 2], z_recv.at[q, 2], 0, z).wait_recv()
            finish(total + rz[q, 2].astype(F32))

    def rs_hooks(q, t):
        @pl.when((t == 1) & (q >= 1))
        def _():
            rs_chip(q - 1)

        @pl.when((t == 4) & (q >= 1))
        def _():
            rs_relay(q - 1)

        @pl.when((t == 6) & (q >= 2))
        def _():
            rs_final(q - 2)

    def rs_begin(q):
        @pl.when(q >= 2)
        def _():
            exchange(q - 2).wait_send()

        for d in range(DEV):
            rows = slice(d * 64, d * 64 + 64)
            pg[q % 2, d % 2, d // 2, 0:64] = ggu[rows, 0:C].astype(BF16)
            pg[q % 2, d % 2, d // 2, 64:128] = ggu[rows, C : 2 * C].astype(BF16)
        turned = gd[...].astype(BF16).T
        for d in range(DEV):
            rows = slice(d * SH, d * SH + SH)
            pg[q % 2, d % 2, d // 2, 128:160] = turned[rows, 0:256]
            pg[q % 2, d % 2, d // 2, 160:192] = turned[rows, 256:512]
        exchange(q).start()

    def prepare(j, forward, input_gradient):
        for d in range(DEV):
            share = wbuf[j, d % 2, d // 2]
            wgu[d * 64 : d * 64 + 64, 0:C] = share[0:64]
            wgu[d * 64 : d * 64 + 64, C : 2 * C] = share[64:128]
            wd[d * SH : d * SH + SH, 0:256] = share[128:160]
            wd[d * SH : d * SH + SH, 256:512] = share[160:192]
        if not forward:
            wdt[...] = wd[...].T
        if input_gradient:
            wt[...] = wgu[...].T

    def tokens(t):
        return pl.ds(pl.multiple_of(t * TB, TB), TB)

    def ag_hooks(j, t):
        @pl.when((t == 1) & (j + 3 < NJ))
        def _():
            stage_two(j + 3)

        @pl.when((t == 4) & (j + 1 < NJ))
        def _():
            stage_three(j + 1)

    sq[...] = jnp.zeros_like(sq)
    copies[1].wait()
    copies[2].wait()

    def first(t, _):
        ts = tokens(t)
        a0[ts] = normed(h1[ts].astype(F32))
        byt[:, ts] = by[ts].T

        @pl.when(t >= NT - 3)
        def _():
            stage_two(t - (NT - 3))

        return 0

    lax.fori_loop(0, NT, first, 0)
    stage_three(0)

    def forward_chunk(k, _):
        from_partner(k).wait_recv()
        prepare(k, True, False)

        def step(t, _):
            ag_hooks(k, t)
            ts = tokens(t)
            gu = dot(a0[ts], wgu[...])
            gate, up = gu[:, :C], gu[:, C:]
            hidden = (gate / (1.0 + jnp.exp(-gate)) * up).astype(BF16)
            part = dot(hidden, wd[...])

            @pl.when(k == 0)
            def _():
                acc[ts] = part

            @pl.when(k != 0)
            def _():
                acc[ts] += part

            return 0

        lax.fori_loop(0, NT, step, 0)
        return 0

    lax.fori_loop(0, NK, forward_chunk, 0)

    def middle(t, _):
        ts = tokens(t)
        h = (h1[ts].astype(F32) + acc[ts].astype(BF16).astype(F32)).astype(BF16)
        h1[ts] = h
        a = normed(h.astype(F32))
        a1[ts] = a
        at[:, ts] = a.T
        return 0

    lax.fori_loop(0, NT, middle, 0)

    def backward(layer, a_ref, k):
        j = layer * NK + k
        q = (1 - layer) * NK + k
        if layer == 1:
            from_partner(j).wait_recv()
        prepare(j, False, layer == 1)
        gd[...] = jnp.zeros_like(gd)
        ggu[...] = jnp.zeros_like(ggu)

        def step(t, _):
            if layer == 1:
                ag_hooks(j, t)
            rs_hooks(q, t)
            ts = tokens(t)
            gu = dot(a_ref[ts], wgu[...])
            by_hidden = dot(by[ts], wdt[...]).astype(BF16).astype(F32)
            gate, up = gu[:, :C], gu[:, C:]
            s = 1.0 / (1.0 + jnp.exp(-gate))
            silu = gate * s
            hidden = (silu * up).astype(BF16)
            by_up = (by_hidden * silu).astype(BF16)
            by_gate = (by_hidden * up * (s + silu * (1.0 - s))).astype(BF16)
            both = jnp.concatenate([by_gate, by_up], axis=1)
            gd[...] += dot(byt[:, ts], hidden)
            ggu[...] += dot(at[:, ts], both)
            if layer == 1:
                part = dot(both, wt[...])

                @pl.when(k == 0)
                def _():
                    acc[ts] = part

                @pl.when(k != 0)
                def _():
                    acc[ts] += part

            return 0

        lax.fori_loop(0, NT, step, 0)
        rs_begin(q)

    lax.fori_loop(0, NK, lambda k, _: (backward(1, a1, k), 0)[1], 0)

    def between(t, _):
        ts = tokens(t)
        wide = h1[ts].astype(F32)
        g = acc[ts].astype(BF16).astype(F32)
        s = lax.rsqrt(jnp.mean(wide * wide, -1, keepdims=True) + 1e-6)
        m = jnp.mean(g * wide, -1, keepdims=True)
        back = (g * s - wide * (s * s * s * m)).astype(BF16)
        total = (back.astype(F32) + by[ts].astype(F32)).astype(BF16)
        by[ts] = total
        byt[:, ts] = total.T
        at[:, ts] = a0[ts].T
        return 0

    lax.fori_loop(0, NT, between, 0)
    lax.fori_loop(0, NK, lambda k, _: (backward(0, a0, k), 0)[1], 0)

    last = jnp.int32(NJ - 1)
    rs_final(last - 1)
    rs_chip(last)
    rs_relay(last)
    rs_final(last)

    def squares(i):
        return pltpu.make_async_remote_copy(
            src_ref=sq, dst_ref=nb.at[i - 1], send_sem=n_send.at[i - 1], recv_sem=n_recv.at[i - 1],
            device_id=(rep, (dp + i) % DEV), device_id_type=MESH)

    for i in range(1, DEV):
        squares(i).start()
    total = sq[...]
    for i in range(1, DEV):
        squares(i).wait_recv()
        total += nb[i - 1]
    sq_out[...] = total
    for i in range(1, DEV):
        squares(i).wait_send()
    for q in (NJ - 2, NJ - 1):
        exchange(q).wait_send()
        wait_z_sends(q)

    def drain(j, _):
        for i in (1, 2, 3):
            along_z(j, i).wait_send()
            for q in (1, 2, 3):
                across(j, i, q).wait_send()
        to_partner(j).wait_send()
        return 0

    lax.fori_loop(0, NJ, drain, 0)


def gradients_of(x, dy, pack):
    vm = pltpu.VMEM
    dma = pltpu.SemaphoreType.DMA
    scratch = [
        vm((NJ, 2, 4, ROWS, C), BF16),
        vm((T, D), BF16),
        vm((T, D), BF16),
        vm((D, T), BF16),
        vm((T, D), BF16),
        vm((D, T), BF16),
        vm((T, D), BF16),
        vm((T, D), F32),
        vm((D, 2 * C), BF16),
        vm((C, D), BF16),
        vm((D, C), BF16),
        vm((2 * C, D), BF16),
        vm((D, C), F32),
        vm((D, 2 * C), F32),
        vm((2, 2, 4, ROWS, C), BF16),
        vm((NJ, 4, ROWS, C), BF16),
        vm((2, 4, ROWS, C), BF16),
        vm((NJ, ROWS, C), BF16),
        vm((NJ, 3, ROWS, C), BF16),
        vm((8, C), F32),
        vm((DEV - 1, 8, C), F32),
        dma((3,)),
        dma((NJ, 3)), dma((NJ, 3)),
        dma((NJ, 3, 3)), dma((NJ, 3, 3)),
        dma((NJ,)), dma((NJ,)),
        dma((NJ,)), dma((NJ,)),
        dma((NJ, 3)), dma((NJ, 3)),
        dma((NJ,)),
        dma((DEV - 1,)), dma((DEV - 1,)),
    ]
    any_space = pl.BlockSpec(memory_space=pl.ANY)
    vmem = pl.BlockSpec(memory_space=pltpu.VMEM)
    return pl.pallas_call(
        kernel,
        out_shape=(jax.ShapeDtypeStruct((NJ, ROWS, C), BF16), jax.ShapeDtypeStruct((8, C), F32)),
        in_specs=[any_space] * 3,
        out_specs=(vmem, vmem),
        scratch_shapes=scratch,
        compiler_params=pltpu.CompilerParams(collective_id=0, has_side_effects=True, vmem_limit_bytes=67_043_328),
    )(x, dy, pack)


def spread(w):
    w = w.reshape(2, 64, DEV, FF // DEV)
    w = jnp.pad(w, ((0, 0), (0, 0), (0, 0), (0, NK * SH - FF // DEV)))
    return w.reshape(2, 64, DEV, NK, SH).transpose(0, 3, 1, 2, 4).reshape(2, NK, 64, C)


def gathered_back(g):
    g = g.reshape(2, NK, 64, DEV, SH).transpose(0, 2, 3, 1, 4).reshape(2, 64, DEV, NK * SH)
    return g[..., : FF // DEV].reshape(2, 64, FF)


def packed(wg, wu, wd):
    down = jnp.pad(wd, ((0, 0), (0, NK * SH - FF // DEV), (0, 0))).reshape(2, NK, SH, 2, C)
    down = down.transpose(0, 1, 3, 2, 4).reshape(2, NK, 2 * SH, C)
    return jnp.concatenate([spread(wg), spread(wu), down], 2).reshape(NJ, ROWS, C)


def unpacked(g):
    g = g.reshape(2, NK, ROWS, C)[::-1]
    down = g[:, :, 128:].reshape(2, NK, 2, SH, C).transpose(0, 1, 3, 2, 4).reshape(2, NK * SH, D)
    return gathered_back(g[:, :, :64]), gathered_back(g[:, :, 64:128]), down[:, : FF // DEV]


def adamw(w, m, v, g):
    m = 0.9 * m + 0.1 * g
    v = 0.95 * v + 0.05 * g * g
    step = m * lax.rsqrt(v + 1e-8) + 0.1 * w
    return (w - 0.02 * step).astype(BF16), m, v


def solution(mesh):
    def step(x, dy, *arrays):
        weights, m, v = (arrays[i : i + 3] for i in (0, 3, 6))
        g, squares = gradients_of(x[0], dy[0], packed(*weights))
        count = 3 * 2 * D * FF
        factor = jnp.minimum(1.0, 0.5 * lax.rsqrt(jnp.sum(squares) / count + 1e-30))
        new = [
            adamw(w.astype(F32), m, v, g.astype(F32) * factor)
            for w, m, v, g in zip(weights, m, v, unpacked(g), strict=True)
        ]
        return tuple(one[which] for which in range(3) for one in new)

    states, cut = P(("rep", "dp"), None, None), P(None, "dp", None)
    return jax.shard_map(
        step,
        mesh=mesh,
        in_specs=(states, states) + (cut,) * 9,
        out_specs=(P("rep", "dp", None),) * 9,
        check_vma=False,
    )
```

time: 488 us -> 241 us (0.49); the launches traced: 478 us -> 240 us
  matrix products: 250 us -> 0 us
  Pallas kernels: 0 us -> 219 us
  waiting for transfers between devices: 160 us -> 0 us
  between operations: 17.3 us -> 1.56 us
  blocking collectives: 14.5 us -> 0 us
  other arithmetic: 17.8 us -> 8.31 us
  local copies, waits for them, and re-layouts: 18.8 us -> 11.6 us
    dot_general x15 -> x0, matrix products: 250 us -> none  [the longest x5 93.5 us: layer(): gate = jnp.dot(a, w['w_gate'], preferred_element_type=jnp.float32)]
    pallas_call x0 -> x1, Pallas kernels: none -> 219 us  [gradients_of(): pl.pallas_call(kernel, out_shape=(jax.ShapeDtypeStruct((NJ, ROWS, C), BF1...]
    reduce_scatter x6 -> x0, waiting for transfers between devices: 97.3 us -> none  [step(): lax.psum_scatter(by_w[name], 'dp', scatter_dimension=0, tiled=True)]
    all_gather x6 -> x0, waiting for transfers between devices: 60.6 us -> none  [fetched(): lax.all_gather(w[number], 'dp', axis=0, tiled=True)]
    psum x1 -> x0, blocking collectives: 14.5 us -> none  [step(): squares = lax.psum(sum((jnp.sum(g * g) for g in gradients)), 'dp')]
    unnamed x30 -> x26, local copies, waits for them, and re-layouts: 13.5 us -> 4.42 us
    reduce_sum x4 -> x1, other arithmetic: 8.46 us -> 1.3 us  [step(): factor = jnp.minimum(1.0, 0.5 * lax.rsqrt(jnp.sum(squares) / count + 1e-30))]
  transfers between devices with their start and end apart: 12 -> 0, of which waited for: 9 -> 0; matrix products, arithmetic and copies ran while one was open for 48% -> 0% of each run, Pallas kernels for 0% -> 0%
where the time goes in v1:
time: 241 us; the launch traced here: 240 us
  Pallas kernels  219 us (91%)
  local copies, waits for them, and re-layouts  11.6 us (5%)
  other arithmetic  8.31 us (3%)
    pallas_call x1, Pallas kernels, gradients_of(): pl.pallas_call(kernel, out_shape=(jax.ShapeDtypeStruct((NJ, ROWS, C), BF1...  219 us
    convert_element_type x3, other arithmetic, adamw(): return ((w - 0.02 * step).astype(BF16), m, v)  5.67 us

profile of v1, /device:TPU:0, one launch (start us, length us, event | category | flops | bytes accessed | tf_op | source)
XLA Modules:
  0.0 240.5 jit_solution(16786073638455434501)
XLA Ops:
  0.6 0.0 copy-start.2
  0.7 1.1 pad.13
  1.7 0.1 reshape.76
  1.8 0.1 copy.28
  1.9 0.0 copy-done.2
  1.9 0.4 copy.24
  2.3 0.2 pad.11
  2.5 0.0 copy-start.4
  2.5 0.1 copy.25
  2.6 0.3 copy.29
  2.8 0.6 copy-done.4
  3.5 0.4 copy.26
  3.8 0.2 pad.12
  4.0 0.1 copy.27
  4.1 0.3 copy.30
  4.4 1.1 pad_maximum_fusion.p_hbm
  5.5 219.0 %shard_map.178 = (bf16[12,192,256]{2,1,0:T(8,128)(2,1)}, f32[8,256]{1,0:T(8,128)}) custom-call(bf16[4096,512]{1,0:T(8,128)(2,1)} %bitcast.32, bf16[4096,512]{1,0:T(8,128)(2,1)} %bitcast.33, bf16[12,192,256]{2,1,0:T(8,128)(2,1)} %pad_maximum_fusion.p_hbm), custom_call_target="tpu_custom_call" | custom-call | tf_op jit(solution)/shard_map/pallas_call | solution.py:424
  224.5 1.3 reduce_sum.9
  226.5 1.3 fusion.15
  227.9 0.4 copy.45
  228.3 0.3 reshape.83
  228.5 0.4 copy.42
  228.9 0.1 slice.28
  229.0 1.0 copy.32
  230.0 0.4 copy.43
  230.4 0.1 slice.31
  230.4 0.0 copy-start
  230.4 0.1 copy.37
  230.5 1.0 copy-done
  231.6 0.2 convert_multiply_fusion
  231.8 1.3 copy.38
  233.1 0.0 copy-start.3
  233.1 0.4 copy.33
  233.5 0.6 copy-done.3
  234.0 0.0 copy-start.1
  234.0 0.0 copy-start.5
  234.1 0.0 copy-start.7
  234.1 0.0 copy-start.8
  234.1 2.8 %fusion.2 = (bf16[2,64,1408]{2,1,0:T(8,128)(2,1)}, f32[2,64,1408]{2,1,0:T(8,128)}, f32[2,64,1408]{2,1,0:T(8,128)}) fusion(bf16[2,64,1408]{2,1,0:T(8,128)(2,1)S(1)} %copy-done.3, f32[2,64,1408]{2,1,0:T(8,128)S(1)} %copy.33, f32[2,64,1408]{2,1,0:T(8,128)} %param.19, f32[2,64,1408]{2,1,0:T(8,128)} %param.16), kind=kLoop, calls=%fused_computation.14 | loop fusion | flops 2703360 | bytes 4325376 | tf_op jit(solution)/shard_map/convert_element_type | solution.py:461
  236.9 0.0 copy-done.1
  236.9 0.0 copy-done.5
  236.9 0.0 copy-done.7
  236.9 0.0 copy-done.8
  236.9 0.0 copy-start.6
  236.9 0.0 copy-start.9
  236.9 0.0 copy-start.10
  237.0 1.4 fusion.5
  238.3 0.0 copy-done.6
  238.3 0.2 copy-done.9
  238.5 0.5 copy-done.10
  239.0 1.4 fusion.8
  (1 shorter events, 0.0 us)
Async XLA Ops:
  0.6 1.2 copy-start.2
  2.5 1.0 copy-start.4
  230.4 1.1 copy-start
  233.1 1.0 copy-start.3
  234.0 2.9 %copy-start.1 = (f32[2,64,1408]{2,1,0:T(8,128)S(1)}, f32[2,64,1408]{2,1,0:T(8,128)}, u32[]{:S(2)}) copy-start(f32[2,64,1408]{2,1,0:T(8,128)} %copy.38) | copy-start | bytes 2162692
  234.0 2.9 %copy-start.5 = (bf16[2,64,1408]{2,1,0:T(8,128)(2,1)S(1)}, bf16[2,64,1408]{2,1,0:T(8,128)(2,1)}, u32[]{:S(2)}) copy-start(bf16[2,64,1408]{2,1,0:T(8,128)(2,1)} %param.14) | copy-start | bytes 1081348
  234.1 2.9 %copy-start.7 = (f32[2,64,1408]{2,1,0:T(8,128)S(1)}, f32[2,64,1408]{2,1,0:T(8,128)}, u32[]{:S(2)}) copy-start(f32[2,64,1408]{2,1,0:T(8,128)} %param.20) | copy-start | bytes 2162692
  234.1 2.9 %copy-start.8 = (f32[2,64,1408]{2,1,0:T(8,128)S(1)}, f32[2,64,1408]{2,1,0:T(8,128)}, u32[]{:S(2)}) copy-start(f32[2,64,1408]{2,1,0:T(8,128)} %param.17) | copy-start | bytes 2162692
  236.9 1.4 copy-start.6
  236.9 1.6 copy-start.9
  236.9 2.1 copy-start.10

commit v2 on v1

v2 whole, which is shorter than its diff:
```python
import functools

import jax
import jax.numpy as jnp
from jax import lax
from jax.experimental import pallas as pl
from jax.experimental.pallas import tpu as pltpu
from jax.sharding import PartitionSpec as P

MESH = pl.DeviceIdType.MESH
F32, BF16 = jnp.float32, jnp.bfloat16
T, D, FF = 4096, 512, 1408
DEV = 8
C = 256
NK = 6
NJ = 2 * NK
SH = C // DEV
SHARE = FF // DEV
ROWS = 192
GATE, UP, LOW, HIGH = slice(0, 64), slice(64, 128), slice(128, 160), slice(160, 192)
LEFT, RIGHT = slice(0, C), slice(C, 2 * C)
TB = 512
NT = T // TB
NT_DIMS = (((1,), (1,)), ((), ()))
RB = 32


def normed(wide):
    scale = lax.rsqrt(jnp.mean(wide * wide, -1, keepdims=True) + 1e-6)
    return (wide * scale).astype(BF16)


def placement(k):
    place, unit = (lax.broadcasted_iota(jnp.int32, (C, FF), axis) for axis in range(2))
    own = k * SH + lax.rem(place, SH)
    return jnp.where((unit == lax.div(place, SH) * SHARE + own) & (own < SHARE), 1.0, 0.0).astype(BF16)


def dot(a, b):
    return jnp.dot(a, b, preferred_element_type=F32)


def kernel(
    x_hbm, dy_hbm, wg, wu, wdown, g_out, sq_out, kept,
    wbuf, a0, a1, at, by, byt, h1, acc, wgu, wd, wdt, wt, gd, ggu, gu, dh, hid, both, pg, rx, tx, rl, rz, sq, nb,
    local_sem, k_sem, s1_send, s1_recv, s2_send, s2_recv, s3_send, s3_recv,
    d_send, d_recv, z_send, z_recv, r_recv, n_send, n_recv,
):
    rep, dp = lax.axis_index("rep"), lax.axis_index("dp")
    z, c = dp // 2, dp % 2
    partner = z * 2 + (1 - c)
    outer = (z == 0) | (z == 3)
    inner = (z == 1) | (z == 2)
    near, far, opposite = 1 + z // 3, 2 - z // 3, 3 - z
    other_outer = 3 * (z - 1)
    other_outer = jnp.where(inner, other_outer, 0)
    far_outer = 3 - other_outer

    copies = [
        pltpu.make_async_copy(x_hbm, h1, local_sem.at[0]),
        pltpu.make_async_copy(dy_hbm, by, local_sem.at[1]),
    ]
    for copy in copies:
        copy.start()
    barrier = pltpu.get_barrier_semaphore()
    for i in range(1, DEV):
        pl.semaphore_signal(barrier, inc=1, device_id=(rep, (dp + i) % DEV), device_id_type=MESH)
    for i in range(1, 4):
        pl.semaphore_signal(barrier, inc=1, device_id=((rep + i) % 4, dp), device_id_type=MESH)

    def quarter(j, zz, rr):
        return wbuf.at[j, c, zz, pl.ds(pl.multiple_of(rr * (ROWS // 4), 16), ROWS // 4)]

    def along_z(j, i):
        ref = quarter(j, z, rep)
        return pltpu.make_async_remote_copy(
            src_ref=ref, dst_ref=ref, send_sem=s1_send.at[j, i - 1], recv_sem=s1_recv.at[j, i - 1],
            device_id=(rep, ((z + i) % 4) * 2 + c), device_id_type=MESH)

    def from_z(j, i):
        ref = quarter(j, (z + 4 - i) % 4, rep)
        return pltpu.make_async_remote_copy(
            src_ref=ref, dst_ref=ref, send_sem=s1_send.at[j, i - 1], recv_sem=s1_recv.at[j, i - 1],
            device_id=(rep, dp), device_id_type=MESH)

    def across(j, i, q):
        ref = quarter(j, (z + 4 - i) % 4, rep)
        return pltpu.make_async_remote_copy(
            src_ref=ref, dst_ref=ref, send_sem=s2_send.at[j, i - 1, q - 1], recv_sem=s2_recv.at[j, i - 1, q - 1],
            device_id=((rep + q) % 4, dp), device_id_type=MESH)

    def from_across(j, i, q):
        ref = quarter(j, (z + 4 - i) % 4, (rep + 4 - q) % 4)
        return pltpu.make_async_remote_copy(
            src_ref=ref, dst_ref=ref, send_sem=s2_send.at[j, i - 1, q - 1], recv_sem=s2_recv.at[j, i - 1, q - 1],
            device_id=(rep, dp), device_id_type=MESH)

    def to_partner(j):
        ref = wbuf.at[j, c]
        return pltpu.make_async_remote_copy(
            src_ref=ref, dst_ref=ref, send_sem=s3_send.at[j], recv_sem=s3_recv.at[j],
            device_id=(rep, partner), device_id_type=MESH)

    def from_partner(j):
        ref = wbuf.at[j, 1 - c]
        return pltpu.make_async_remote_copy(
            src_ref=ref, dst_ref=ref, send_sem=s3_send.at[j], recv_sem=s3_recv.at[j],
            device_id=(rep, dp), device_id_type=MESH)

    def stage_one(j):
        for i in (1, 2, 3):
            along_z(j, i).start()

    def stage_two(j):
        for i in (1, 2, 3):
            from_z(j, i).wait_recv()
            for q in (1, 2, 3):
                across(j, i, q).start()

    def stage_three(j):
        for i in (1, 2, 3):
            for q in (1, 2, 3):
                from_across(j, i, q).wait_recv()
        to_partner(j).start()

    def pack(k):
        places = placement(k)
        for part, w in ((GATE, wg), (UP, wu)):
            moved = lax.dot_general(w[...].reshape(-1, FF), places, NT_DIMS, preferred_element_type=F32).astype(BF16)
            for layer in range(2):
                wbuf[layer * NK + k, c, z, part] = moved[layer * 64 : layer * 64 + 64]
        have = min(SH, SHARE - k * SH)
        for layer in range(2):
            rows = wdown[layer, k * SH : k * SH + have]
            if have < SH:
                rows = jnp.concatenate([rows, jnp.zeros((SH - have, D), BF16)])
            wbuf[layer * NK + k, c, z, LOW] = rows[:, LEFT]
            wbuf[layer * NK + k, c, z, HIGH] = rows[:, RIGHT]

    pack(0)
    pl.semaphore_wait(barrier, DEV - 1 + 3)
    for k in range(1, NK):
        pack(k)
        stage_one(k - 1)
    lax.fori_loop(NK - 1, NJ, lambda j, _: (stage_one(j), 0)[1], 0)

    def exchange(q):
        return pltpu.make_async_remote_copy(
            src_ref=pg.at[q % 2, 1 - c], dst_ref=rx.at[q % 4], send_sem=d_send.at[q], recv_sem=d_recv.at[q],
            device_id=(rep, partner), device_id_type=MESH)

    def z_copy(q, block, dst, recv_sem, n, zz):
        return pltpu.make_async_remote_copy(
            src_ref=tx.at[q % 2, block], dst_ref=dst, send_sem=z_send.at[q, n], recv_sem=recv_sem,
            device_id=(rep, zz * 2 + c), device_id_type=MESH)

    def chip_sum(q, block):
        return pg[q % 2, c, block].astype(F32) + rx[q % 4, block].astype(F32)

    def wait_z_sends(q):
        for n in range(3):
            z_copy(q, 0, rz.at[q % 4, 0], z_recv.at[q, 0], n, z).wait_send()

    def rs_chip(q):
        exchange(q).wait_recv()

        @pl.when(q >= 2)
        def _():
            wait_z_sends(q - 2)

        for block in range(4):
            tx[q % 2, block] = chip_sum(q, block).astype(BF16)

        @pl.when(outer)
        def _():
            z_copy(q, opposite, rl.at[q % 4], r_recv.at[q], 0, near).start()
            z_copy(q, far, rz.at[q % 4, 1], z_recv.at[q, 1], 1, far).start()
            z_copy(q, near, rz.at[q % 4, 0], z_recv.at[q, 0], 2, near).start()

        @pl.when(inner)
        def _():
            z_copy(q, opposite, rz.at[q % 4, 2], z_recv.at[q, 2], 0, opposite).start()
            z_copy(q, other_outer, rz.at[q % 4, 0], z_recv.at[q, 0], 1, other_outer).start()

    def rs_relay(q):
        @pl.when(inner)
        def _():
            z_copy(q, 0, rl.at[q % 4], r_recv.at[q], 2, z).wait_recv()
            tx[q % 2, far_outer] = (chip_sum(q, far_outer) + rl[q % 4].astype(F32)).astype(BF16)
            z_copy(q, far_outer, rz.at[q % 4, 1], z_recv.at[q, 1], 2, far_outer).start()

    def rs_final(q):
        for n in range(2):
            z_copy(q, 0, rz.at[q % 4, n], z_recv.at[q, n], 0, z).wait_recv()
        total = chip_sum(q, z) + rz[q % 4, 0].astype(F32) + rz[q % 4, 1].astype(F32)

        def finish(value):
            rounded = value.astype(BF16)
            g_out[q] = rounded
            wide = rounded.astype(F32)
            sq[...] += jnp.sum((wide * wide).reshape(ROWS // 8, 8, C), 0)

        @pl.when(outer)
        def _():
            finish(total)

        @pl.when(inner)
        def _():
            z_copy(q, 0, rz.at[q % 4, 2], z_recv.at[q, 2], 0, z).wait_recv()
            finish(total + rz[q % 4, 2].astype(F32))

    def rs_begin(q):
        @pl.when(q >= 2)
        def _():
            exchange(q - 2).wait_send()

        for d in range(DEV):
            rows = slice(d * 64, d * 64 + 64)
            pg[q % 2, d % 2, d // 2, GATE] = ggu[rows, LEFT].astype(BF16)
            pg[q % 2, d % 2, d // 2, UP] = ggu[rows, RIGHT].astype(BF16)
        turned = gd[...].astype(BF16).T
        for d in range(DEV):
            rows = slice(d * SH, d * SH + SH)
            pg[q % 2, d % 2, d // 2, LOW] = turned[rows, LEFT]
            pg[q % 2, d % 2, d // 2, HIGH] = turned[rows, RIGHT]
        exchange(q).start()

    def load_gate_up(j):
        for d in range(DEV):
            rows = slice(d * 64, d * 64 + 64)
            wgu[rows, LEFT] = wbuf[j, d % 2, d // 2, GATE]
            wgu[rows, RIGHT] = wbuf[j, d % 2, d // 2, UP]

    def load_down(j):
        for d in range(DEV):
            rows = slice(d * SH, d * SH + SH)
            wd[rows, LEFT] = wbuf[j, d % 2, d // 2, LOW]
            wd[rows, RIGHT] = wbuf[j, d % 2, d // 2, HIGH]

    def tokens(t):
        return pl.ds(pl.multiple_of(t * TB, TB), TB)

    def ag_two(j):
        @pl.when(j + 3 < NJ)
        def _():
            stage_two(j + 3)

    def ag_three(j):
        @pl.when(j + 1 < NJ)
        def _():
            stage_three(j + 1)

    sq[...] = jnp.zeros_like(sq)
    for copy in copies:
        copy.wait()

    def first(t, _):
        ts = tokens(t)
        a0[ts] = normed(h1[ts].astype(F32))
        byt[:, ts] = by[ts].T
        acc[ts] = jnp.zeros((TB, D), F32)

        @pl.when(t >= NT - 3)
        def _():
            stage_two(t - (NT - 3))

        return 0

    lax.fori_loop(0, NT, first, 0)
    stage_three(0)

    def together(*lists):
        order = sorted((n / len(one), m, n) for m, one in enumerate(lists) for n in range(len(one)))
        for _, m, n in order:
            lists[m][n]()

    def gate_up(a_ref, t, slot):
        def product(n):
            cols = slice(n * C, n * C + C)
            gu[slot, :, cols] = dot(a_ref[tokens(t)], wgu[:, cols])

        return [functools.partial(product, n) for n in range(2)]

    def of_hidden(t, slot):
        def product():
            dh[slot] = dot(by[tokens(t)], wdt[...]).astype(BF16)

        return [product]

    def elementwise(gu_slot, slot, hidden_gradient):
        def piece(n):
            rows = slice(n * RB, n * RB + RB)
            gate, up = gu[gu_slot, rows, LEFT], gu[gu_slot, rows, RIGHT]
            s = 1.0 / (1.0 + jnp.exp(-gate))
            silu = gate * s
            hid[slot, rows] = (silu * up).astype(BF16)
            if hidden_gradient:
                by_hidden = dh[slot, rows].astype(F32)
                both[slot, rows, RIGHT] = (by_hidden * silu).astype(BF16)
                both[slot, rows, LEFT] = (by_hidden * up * (s + silu * (1.0 - s))).astype(BF16)

        return [functools.partial(piece, n) for n in range(TB // RB)]

    def forward_products(t, slot):
        ts = tokens(t)

        def down(n):
            cols = slice(n * C, n * C + C)
            acc[ts, cols] += dot(hid[slot], wd[:, cols])

        return [functools.partial(down, n) for n in range(2)]

    def last_products(t, slot, input_gradient):
        ts = tokens(t)

        def of_down():
            gd[...] += dot(byt[:, ts], hid[slot])

        def of_gate_up(n):
            cols = slice(n * C, n * C + C)
            ggu[:, cols] += dot(at[:, ts], both[slot, :, cols])

        def of_input(n):
            cols = slice(n * C, n * C + C)
            acc[ts, cols] += dot(both[slot], wt[:, cols])

        parts = [of_down] + [functools.partial(of_gate_up, n) for n in range(2)]
        return parts + [functools.partial(of_input, n) for n in range(2)] if input_gradient else parts

    def run(j0, for_one, for_three, one, two, three, hook, finish):
        for_one(j0)
        together(one(j0, 0))
        together(one(j0, 1), two(j0, 0))
        for_three(j0)

        def chunk(k, _):
            j = j0 + k
            following = j0 + jnp.minimum(k + 1, NK - 1)
            for t in range(1, NT - 1):
                if t % 2:
                    hook(k, t // 2)
                together(one(j, t + 1), two(j, t), three(t - 1))
            hook(k, NT // 2 - 1)
            for_one(following)
            together(one(following, 0), two(j, NT - 1), three(NT - 2))
            together(one(following, 1), two(following, 0), three(NT - 1))
            finish(k)
            for_three(following)
            return 0

        lax.fori_loop(0, NK, chunk, 0)

    def keep(k, t):
        return pltpu.make_async_copy(gu.at[t % 4], kept.at[k, t], k_sem.at[t % 4])

    def fetch(k, t):
        return pltpu.make_async_copy(kept.at[k, t], gu.at[t % 4], k_sem.at[t % 4])

    def arrive(j):
        from_partner(j).wait_recv()

    def forward_hook(k, n):
        if n == 0:
            ag_two(k)
        if n == 1:
            ag_three(k)
        if n == 3:
            arrive(k + 1)

    def forward_one(k, t):
        def free():
            keep(k, t).wait()

        parts = gate_up(a0, t, t % 4)
        return parts if isinstance(k, int) else [free] + parts

    def forward_two(k, t):
        parts = elementwise(t % 4, t % 2, False)
        return parts[:4] + [keep(k, t).start] + parts[4:]

    arrive(0)
    for t in (2, 3):
        gu[t] = jnp.zeros((TB, 2 * C), F32)
        keep(0, t).start()
    run(
        0, load_gate_up, load_down,
        forward_one, forward_two,
        lambda t: forward_products(t, t % 2),
        forward_hook,
        lambda k: None,
    )
    for t in (0, 2, 3):
        keep(0, t).wait()

    def middle(t, _):
        ts = tokens(t)
        h = (h1[ts].astype(F32) + acc[ts].astype(BF16).astype(F32)).astype(BF16)
        acc[ts] = jnp.zeros((TB, D), F32)
        h1[ts] = h
        a = normed(h.astype(F32))
        a1[ts] = a
        at[:, ts] = a.T
        return 0

    lax.fori_loop(0, NT, middle, 0)

    def backward(layer):
        j0, q0 = layer * NK, (1 - layer) * NK

        def for_one(j):
            if layer == 1:
                load_gate_up(j)
            load_down(j)
            wdt[...] = wd[...].T

        def for_three(j):
            if layer == 1:
                wt[...] = wgu[...].T

        def hook(k, n):
            j, q = j0 + k, q0 + k
            if layer == 1 and n == 0:
                ag_two(j)
            if layer == 1 and n == 1:
                ag_three(j)
            if layer == 1 and n == 3:
                @pl.when(k + 1 < NK)
                def _():
                    arrive(j + 1)

            @pl.when(q >= 1)
            def _():
                if n == 1:
                    rs_chip(q - 1)
                if n == 3:
                    rs_relay(q - 1)

            @pl.when(q >= 2)
            def _():
                if n == 2:
                    rs_final(q - 2)

        def clear():
            gd[...] = jnp.zeros_like(gd)
            ggu[...] = jnp.zeros_like(ggu)

        def finish(k):
            rs_begin(q0 + k)
            clear()

        clear()
        if layer == 1:
            run(
                j0, for_one, for_three,
                lambda j, t: gate_up(a1, t, t % 4) + of_hidden(t, t % 2),
                lambda j, t: elementwise(t % 4, t % 2, True),
                lambda t: last_products(t, t % 2, True),
                hook,
                finish,
            )
        else:
            def two(k, t):
                ahead = t + 3
                after = k if ahead < NT else jnp.minimum(k + 1, NK - 1)
                parts = elementwise(t % 4, t % 2, True)
                return [fetch(after, ahead % NT).start, fetch(k, t).wait] + parts

            run(
                0, for_one, for_three,
                lambda k, t: of_hidden(t, t % 2),
                two,
                lambda t: last_products(t, t % 2, False),
                hook,
                finish,
            )
            for t in (1, 2, 3):
                fetch(0, t).wait()

    backward(1)

    def between(t, _):
        ts = tokens(t)
        wide = h1[ts].astype(F32)
        g = acc[ts].astype(BF16).astype(F32)
        s = lax.rsqrt(jnp.mean(wide * wide, -1, keepdims=True) + 1e-6)
        m = jnp.mean(g * wide, -1, keepdims=True)
        back = (g * s - wide * (s * s * s * m)).astype(BF16)
        total = (back.astype(F32) + by[ts].astype(F32)).astype(BF16)
        by[ts] = total
        byt[:, ts] = total.T
        at[:, ts] = a0[ts].T
        return 0

    for t in range(3):
        fetch(0, t).start()
    lax.fori_loop(0, NT, between, 0)
    backward(0)

    last = jnp.int32(NJ - 1)
    rs_final(last - 1)
    rs_chip(last)
    rs_relay(last)
    rs_final(last)

    def squares(i):
        return pltpu.make_async_remote_copy(
            src_ref=sq, dst_ref=nb.at[i - 1], send_sem=n_send.at[i - 1], recv_sem=n_recv.at[i - 1],
            device_id=(rep, (dp + i) % DEV), device_id_type=MESH)

    for i in range(1, DEV):
        squares(i).start()
    total = sq[...]
    for i in range(1, DEV):
        squares(i).wait_recv()
        total += nb[i - 1]
    sq_out[...] = total
    for i in range(1, DEV):
        squares(i).wait_send()
    for q in (NJ - 2, NJ - 1):
        exchange(q).wait_send()
        wait_z_sends(q)

    def drain(j, _):
        for i in (1, 2, 3):
            along_z(j, i).wait_send()
            for q in (1, 2, 3):
                across(j, i, q).wait_send()
        to_partner(j).wait_send()
        return 0

    lax.fori_loop(0, NJ, drain, 0)


def gradients_of(x, dy, *weights):
    vm = pltpu.VMEM
    dma = pltpu.SemaphoreType.DMA
    scratch = [
        vm((NJ, 2, 4, ROWS, C), BF16),
        vm((T, D), BF16),
        vm((T, D), BF16),
        vm((D, T), BF16),
        vm((T, D), BF16),
        vm((D, T), BF16),
        vm((T, D), BF16),
        vm((T, D), F32),
        vm((D, 2 * C), BF16),
        vm((C, D), BF16),
        vm((D, C), BF16),
        vm((2 * C, D), BF16),
        vm((D, C), F32),
        vm((D, 2 * C), F32),
        vm((4, TB, 2 * C), F32),
        vm((2, TB, C), BF16),
        vm((2, TB, C), BF16),
        vm((2, TB, 2 * C), BF16),
        vm((2, 2, 4, ROWS, C), BF16),
        vm((4, 4, ROWS, C), BF16),
        vm((2, 4, ROWS, C), BF16),
        vm((4, ROWS, C), BF16),
        vm((4, 3, ROWS, C), BF16),
        vm((8, C), F32),
        vm((DEV - 1, 8, C), F32),
        dma((2,)), dma((4,)),
        dma((NJ, 3)), dma((NJ, 3)),
        dma((NJ, 3, 3)), dma((NJ, 3, 3)),
        dma((NJ,)), dma((NJ,)),
        dma((NJ,)), dma((NJ,)),
        dma((NJ, 3)), dma((NJ, 3)),
        dma((NJ,)),
        dma((DEV - 1,)), dma((DEV - 1,)),
    ]
    any_space = pl.BlockSpec(memory_space=pl.ANY)
    vmem = pl.BlockSpec(memory_space=pltpu.VMEM)
    return pl.pallas_call(
        kernel,
        out_shape=(jax.ShapeDtypeStruct((NJ, ROWS, C), BF16), jax.ShapeDtypeStruct((8, C), F32),
                   jax.ShapeDtypeStruct((NK, NT, TB, 2 * C), F32)),
        in_specs=[any_space] * 2 + [vmem] * 3,
        out_specs=(vmem, vmem, any_space),
        scratch_shapes=scratch,
        compiler_params=pltpu.CompilerParams(collective_id=0, has_side_effects=True, vmem_limit_bytes=67_043_328),
    )(x, dy, *weights)


def adamw(w, m, v, g):
    m = 0.9 * m + 0.1 * g
    v = 0.95 * v + 0.05 * g * g
    step = m * lax.rsqrt(v + 1e-8) + 0.1 * w
    return (w - 0.02 * step).astype(BF16), m, v


def update(g, squares, *refs):
    ins, outs, held, (places, came, in_sem, out_sem) = refs[:9], refs[9:18], refs[18:27], refs[27:]
    copies = [pltpu.make_async_copy(a, b, in_sem.at[n]) for n, (a, b) in enumerate(zip(ins, held))]
    puts = [pltpu.make_async_copy(b, a, out_sem.at[n]) for n, (a, b) in enumerate(zip(outs, held))]
    for copy in copies:
        copy.start()
    for k in range(NK):
        places[k * C : k * C + C] = placement(k)
    count = 3 * 2 * D * FF
    factor = jnp.minimum(1.0, 0.5 * lax.rsqrt(jnp.sum(squares[...], keepdims=True) / count + 1e-30))
    chunks = [
        jnp.concatenate([g[NK + k, GATE], g[NK + k, UP], g[k, GATE], g[k, UP]]) for k in range(NK)
    ]
    came[...] = dot(jnp.concatenate(chunks, 1), places[...])
    for n in range(3):
        for which in range(n, 9, 3):
            copies[which].wait()
        w, m, v = held[n::3]
        step = SH // 2
        for layer in range(2):
            for row in range(0, w.shape[1], step):
                rows = slice(row, row + step)
                if n < 2:
                    first = (layer * 2 + n) * 64 + row
                    part = came[first : first + step]
                else:
                    q, inside = (1 - layer) * NK + row // SH, row % SH
                    part = jnp.concatenate(
                        [g[q, one.start + inside : one.start + inside + step] for one in (LOW, HIGH)], 1
                    ).astype(F32)
                w[layer, rows], m[layer, rows], v[layer, rows] = adamw(
                    w[layer, rows].astype(F32), m[layer, rows], v[layer, rows], part * factor
                )
        for which in range(n, 9, 3):
            puts[which].start()
    for put in puts:
        put.wait()


def updated(g, squares, arrays):
    any_space, vmem = pl.BlockSpec(memory_space=pl.ANY), pl.BlockSpec(memory_space=pltpu.VMEM)
    like = [jax.ShapeDtypeStruct(a.shape, a.dtype) for a in arrays]
    return pl.pallas_call(
        update,
        out_shape=like,
        in_specs=[vmem] * 2 + [any_space] * 9,
        out_specs=[any_space] * 9,
        scratch_shapes=[pltpu.VMEM(a.shape, a.dtype) for a in arrays]
        + [
            pltpu.VMEM((NK * C, FF), BF16),
            pltpu.VMEM((4 * 64, FF), F32),
            pltpu.SemaphoreType.DMA((9,)),
            pltpu.SemaphoreType.DMA((9,)),
        ],
        compiler_params=pltpu.CompilerParams(vmem_limit_bytes=60_000_000),
    )(g, squares, *arrays)


def solution(mesh):
    def step(x, dy, *arrays):
        g, squares, _ = gradients_of(x[0], dy[0], *arrays[:3])
        return tuple(updated(g, squares, arrays))

    states, cut = P(("rep", "dp"), None, None), P(None, "dp", None)
    return jax.shard_map(
        step,
        mesh=mesh,
        in_specs=(states, states) + (cut,) * 9,
        out_specs=(P("rep", "dp", None),) * 9,
        check_vma=False,
    )
```

time: 241 us -> 205 us (0.85)
  Pallas kernels: 219 us -> 204 us
  local copies, waits for them, and re-layouts: 11.6 us -> 0 us
  other arithmetic: 8.31 us -> 0 us
    pallas_call x1, Pallas kernels: 219 us -> 197 us  [gradients_of(): pl.pallas_call(kernel, out_shape=(jax.ShapeDtypeStruct((NJ, ROWS, C), BF1...]
    pallas_call x0 -> x1, Pallas kernels: none -> 6.9 us  [updated(): pl.pallas_call(update, out_shape=like, in_specs=[vmem] * 2 + [any_space]...]
    convert_element_type x3 -> x0, other arithmetic: 5.67 us -> none  [adamw(): return ((w - 0.02 * step).astype(BF16), m, v)]
    unnamed x26 -> x0, local copies, waits for them, and re-layouts: 4.42 us -> none
where the time goes in v2:
time: 205 us
  Pallas kernels  204 us (100%)
    pallas_call x1, Pallas kernels, gradients_of(): pl.pallas_call(kernel, out_shape=(jax.ShapeDtypeStruct((NJ, ROWS, C), BF1...  197 us
    pallas_call x1, Pallas kernels, updated(): pl.pallas_call(update, out_shape=like, in_specs=[vmem] * 2 + [any_space]...  6.9 us

profile of v2, /device:TPU:0, one launch (start us, length us, event | category | flops | bytes accessed | tf_op | source)
XLA Modules:
  0.0 205.1 jit_solution(175305950747924162)
XLA Ops:
  0.6 197.3 %shard_map.178 = (bf16[12,192,256]{2,1,0:T(8,128)(2,1)}, f32[8,256]{1,0:T(8,128)}, f32[6,8,512,512]{3,2,1,0:T(8,128)}) custom-call(bf16[4096,512]{1,0:T(8,128)(2,1)} %bitcast.2, bf16[4096,512]{1,0:T(8,128)(2,1)} %bitcast.3, bf16[2,64,1408]{2,1,0:T(8,128)(2,1)} %refs_0_.1, bf16[2,64,1408]{2,1,0:T(8,128)(2,1)} %refs_1_.1, bf16[2,176,512]{2,1,0:T(8,128)(2,1)} %refs_2_.1), custom_call_target="tpu_custom_call" | custom-call | tf_op jit(solution)/shard_map/pallas_call | solution.py:574
  198.0 6.9 %shard_map.179 = (bf16[2,64,1408]{2,1,0:T(8,128)(2,1)}, bf16[2,64,1408]{2,1,0:T(8,128)(2,1)}, bf16[2,176,512]{2,1,0:T(8,128)(2,1)}, f32[2,64,1408]{2,1,0:T(8,128...) custom-call(bf16[12,192,256]{2,1,0:T(8,128)(2,1)} %get-tuple-element, ...), custom_call_target="tpu_custom_call" | custom-call | tf_op jit(solution)/shard_map/pallas_call | solution.py:634

commit v3 on v2

--- a/solution.py
+++ b/solution.py
@@ -146,16 +146,16 @@
 
     def exchange(q):
         return pltpu.make_async_remote_copy(
-            src_ref=pg.at[q % 2, 1 - c], dst_ref=rx.at[q % 4], send_sem=d_send.at[q], recv_sem=d_recv.at[q],
+            src_ref=pg.at[q % 3, 1 - c], dst_ref=rx.at[q % 4], send_sem=d_send.at[q], recv_sem=d_recv.at[q],
             device_id=(rep, partner), device_id_type=MESH)
 
     def z_copy(q, block, dst, recv_sem, n, zz):
         return pltpu.make_async_remote_copy(
-            src_ref=tx.at[q % 2, block], dst_ref=dst, send_sem=z_send.at[q, n], recv_sem=recv_sem,
+            src_ref=tx.at[q % 3, block], dst_ref=dst, send_sem=z_send.at[q, n], recv_sem=recv_sem,
             device_id=(rep, zz * 2 + c), device_id_type=MESH)
 
     def chip_sum(q, block):
-        return pg[q % 2, c, block].astype(F32) + rx[q % 4, block].astype(F32)
+        return pg[q % 3, c, block].astype(F32) + rx[q % 4, block].astype(F32)
 
     def wait_z_sends(q):
         for n in range(3):
@@ -164,12 +164,12 @@
     def rs_chip(q):
         exchange(q).wait_recv()
 
-        @pl.when(q >= 2)
-        def _():
-            wait_z_sends(q - 2)
+        @pl.when(q >= 3)
+        def _():
+            wait_z_sends(q - 3)
 
         for block in range(4):
-            tx[q % 2, block] = chip_sum(q, block).astype(BF16)
+            tx[q % 3, block] = chip_sum(q, block).astype(BF16)
 
         @pl.when(outer)
         def _():
@@ -186,7 +186,7 @@
         @pl.when(inner)
         def _():
             z_copy(q, 0, rl.at[q % 4], r_recv.at[q], 2, z).wait_recv()
-            tx[q % 2, far_outer] = (chip_sum(q, far_outer) + rl[q % 4].astype(F32)).astype(BF16)
+            tx[q % 3, far_outer] = (chip_sum(q, far_outer) + rl[q % 4].astype(F32)).astype(BF16)
             z_copy(q, far_outer, rz.at[q % 4, 1], z_recv.at[q, 1], 2, far_outer).start()
 
     def rs_final(q):
@@ -210,19 +210,19 @@
             finish(total + rz[q % 4, 2].astype(F32))
 
     def rs_begin(q):
-        @pl.when(q >= 2)
-        def _():
-            exchange(q - 2).wait_send()
+        @pl.when(q >= 3)
+        def _():
+            exchange(q - 3).wait_send()
 
         for d in range(DEV):
             rows = slice(d * 64, d * 64 + 64)
-            pg[q % 2, d % 2, d // 2, GATE] = ggu[rows, LEFT].astype(BF16)
-            pg[q % 2, d % 2, d // 2, UP] = ggu[rows, RIGHT].astype(BF16)
+            pg[q % 3, d % 2, d // 2, GATE] = ggu[rows, LEFT].astype(BF16)
+            pg[q % 3, d % 2, d // 2, UP] = ggu[rows, RIGHT].astype(BF16)
         turned = gd[...].astype(BF16).T
         for d in range(DEV):
             rows = slice(d * SH, d * SH + SH)
-            pg[q % 2, d % 2, d // 2, LOW] = turned[rows, LEFT]
-            pg[q % 2, d % 2, d // 2, HIGH] = turned[rows, RIGHT]
+            pg[q % 3, d % 2, d // 2, LOW] = turned[rows, LEFT]
+            pg[q % 3, d % 2, d // 2, HIGH] = turned[rows, RIGHT]
         exchange(q).start()
 
     def load_gate_up(j):
@@ -428,17 +428,19 @@
                 def _():
                     arrive(j + 1)
 
-            @pl.when(q >= 1)
-            def _():
-                if n == 1:
+            if n == 0:
+                @pl.when(q >= 2)
+                def _():
+                    rs_relay(q - 2)
+
+                @pl.when(q >= 3)
+                def _():
+                    rs_final(q - 3)
+
+            if n == 1:
+                @pl.when(q >= 1)
+                def _():
                     rs_chip(q - 1)
-                if n == 3:
-                    rs_relay(q - 1)
-
-            @pl.when(q >= 2)
-            def _():
-                if n == 2:
-                    rs_final(q - 2)
 
         def clear():
             gd[...] = jnp.zeros_like(gd)
@@ -497,8 +499,10 @@
     backward(0)
 
     last = jnp.int32(NJ - 1)
+    rs_relay(last - 1)
+    rs_final(last - 2)
+    rs_chip(last)
     rs_final(last - 1)
-    rs_chip(last)
     rs_relay(last)
     rs_final(last)
 
@@ -516,7 +520,7 @@
     sq_out[...] = total
     for i in range(1, DEV):
         squares(i).wait_send()
-    for q in (NJ - 2, NJ - 1):
+    for q in range(NJ - 3, NJ):
         exchange(q).wait_send()
         wait_z_sends(q)
 
@@ -553,9 +557,9 @@
         vm((2, TB, C), BF16),
         vm((2, TB, C), BF16),
         vm((2, TB, 2 * C), BF16),
-        vm((2, 2, 4, ROWS, C), BF16),
+        vm((3, 2, 4, ROWS, C), BF16),
         vm((4, 4, ROWS, C), BF16),
-        vm((2, 4, ROWS, C), BF16),
+        vm((3, 4, ROWS, C), BF16),
         vm((4, ROWS, C), BF16),
         vm((4, 3, ROWS, C), BF16),
         vm((8, C), F32),

time: 205 us -> 199 us (0.971)
  Pallas kernels: 204 us -> 198 us
    pallas_call x1, Pallas kernels: 197 us -> 191 us  [gradients_of(): pl.pallas_call(kernel, out_shape=(jax.ShapeDtypeStruct((NJ, ROWS, C), BF1...]
where the time goes in v3:
time: 199 us
  Pallas kernels  198 us (99%)
    pallas_call x1, Pallas kernels, gradients_of(): pl.pallas_call(kernel, out_shape=(jax.ShapeDtypeStruct((NJ, ROWS, C), BF1...  191 us
    pallas_call x1, Pallas kernels, updated(): pl.pallas_call(update, out_shape=like, in_specs=[vmem] * 2 + [any_space]...  6.91 us

profile of v3, /device:TPU:0, one launch (start us, length us, event | category | flops | bytes accessed | tf_op | source)
XLA Modules:
  0.0 198.9 jit_solution(896973657797522104)
XLA Ops:
  0.6 191.2 %shard_map.178 = (bf16[12,192,256]{2,1,0:T(8,128)(2,1)}, f32[8,256]{1,0:T(8,128)}, f32[6,8,512,512]{3,2,1,0:T(8,128)}) custom-call(bf16[4096,512]{1,0:T(8,128)(2,1)} %bitcast.2, bf16[4096,512]{1,0:T(8,128)(2,1)} %bitcast.3, bf16[2,64,1408]{2,1,0:T(8,128)(2,1)} %refs_0_.1, bf16[2,64,1408]{2,1,0:T(8,128)(2,1)} %refs_1_.1, bf16[2,176,512]{2,1,0:T(8,128)(2,1)} %refs_2_.1), custom_call_target="tpu_custom_call" | custom-call | tf_op jit(solution)/shard_map/pallas_call | solution.py:578
  191.8 6.9 %shard_map.179 = (bf16[2,64,1408]{2,1,0:T(8,128)(2,1)}, bf16[2,64,1408]{2,1,0:T(8,128)(2,1)}, bf16[2,176,512]{2,1,0:T(8,128)(2,1)}, f32[2,64,1408]{2,1,0:T(8,128...) custom-call(bf16[12,192,256]{2,1,0:T(8,128)(2,1)} %get-tuple-element, ...), custom_call_target="tpu_custom_call" | custom-call | tf_op jit(solution)/shard_map/pallas_call | solution.py:638
